TPU v7x, 8 devices: a whole 2x2x1 slice. The times are simulated.
8 devices in a mesh: data: 1 (over z), pipe: 8 (over y, x, core).
Axes of the slice: x: 2, y: 2, z: 1, core: 2. Of those that a mesh axis runs over, the one named last changes fastest.
Arguments:
- x_slice: bfloat16 [2048, 2048], P(('data', 'pipe'))
- slice_idx: int32 [8], P(('data', 'pipe'))
- k_cache: bfloat16 [30720, 24, 128], P(('data', 'pipe'))
- v_cache: bfloat16 [30720, 24, 128], P(('data', 'pipe'))
- w_q: bfloat16 [8, 2048, 3072], P('pipe')
- w_kv: bfloat16 [8, 2048, 6144], P('pipe')
- w_o: bfloat16 [8, 3072, 2048], P('pipe')
- w_gate: bfloat16 [8, 2048, 8192], P('pipe')
- w_up: bfloat16 [8, 2048, 8192], P('pipe')
- w_down: bfloat16 [8, 8192, 2048], P('pipe')
Outputs:
- output 1: bfloat16 [2048, 2048], P(('data', 'pipe'))
- output 2: float32 [2048, 24], P(('data', 'pipe'))
All inputs are finite; a program needn't handle non-finite values.
Results may differ from a plain program's by a relative error of at most 0.00906081.
Values are sent between devices in bfloat16 or wider.
A program may use at most 1 GiB of HBM per device.

v0:
```python
import math

import jax
import jax.numpy as jnp
from jax import lax
from jax.experimental import pallas as pl
from jax.experimental.pallas import tpu as pltpu
from jax.sharding import PartitionSpec as P

BF = jnp.bfloat16
F32 = jnp.float32
HD = 128
TN = 512
TK = 2048
RING = 12
RAW = 3
KB = 256
G = 4
FLOOR = -1e30
LIMIT = 2.0 ** 15
HBM = pl.BlockSpec(memory_space=pltpu.HBM)
SM = pl.BlockSpec(memory_space=pltpu.SMEM)


def rms(values):
    v = values.astype(F32)
    return (v * lax.rsqrt(jnp.mean(v * v, axis=-1, keepdims=True) + 1e-6)).astype(BF)


def dot(a, b):
    return jnp.dot(a, b, preferred_element_type=F32)


def layer_kernel(idx_ref, x_hbm, k_hbm, v_hbm, wq, wkv, wo, wg, wu, wd, y_hbm, lse_hbm,
                 ring, kraw, vraw, kt, vt, kn, vn, qa, acc, pb, mu_s, l_s, lb_s,
                 x_s, a_s, o_s, h_s, y_s, lse_s, wsem, ksem, msem):
    n = idx_ref[0]
    rows, dm = x_s.shape
    heads = qa.shape[0]
    c = HD ** -0.5 * math.log2(math.e)
    log2 = math.log(2.0)

    def col(i, w=TN):
        return pl.ds(pl.multiple_of(i * w, w), w)

    def fetch(e, src, height=TK):
        s = lax.rem(e, RING)
        pltpu.make_async_copy(src, ring.at[s, pl.ds(0, height)], wsem.at[s]).start()

    def ready(e, height=TK):
        s = lax.rem(e, RING)
        pltpu.make_async_copy(wg.at[pl.ds(0, height), pl.ds(0, TN)], ring.at[s, pl.ds(0, height)], wsem.at[s]).wait()
        return s

    def fetch_wo(e, nt):
        fetch(e, wo.at[pl.ds(0, TK), col(nt)])
        fetch(e + 1, wo.at[pl.ds(TK, wo.shape[0] - TK), col(nt)], wo.shape[0] - TK)

    def fetch_gu(e, nt):
        fetch(e, wg.at[:, col(nt)])
        fetch(e + 1, wu.at[:, col(nt)])

    def fetch_wd(e, j):
        for d in range(2):
            jj = j + d
            fetch(e + d, wd.at[col(lax.rem(jj, 4), TK), col(lax.div(jj, 4))])

    xcopy = pltpu.make_async_copy(x_hbm, x_s, msem.at[0])
    xcopy.start()
    for e in range(6):
        fetch(e, wq.at[:, pl.ds(e * TN, TN)])
    for e in range(6, RING):
        fetch(e, wkv.at[:, pl.ds((e - 6) * TN, TN)])

    def kv_copies(b):
        s = lax.rem(b, RAW)
        return [
            pltpu.make_async_copy(k_hbm.at[pl.ds(b * KB, KB)], kraw.at[s], ksem.at[s, 0]),
            pltpu.make_async_copy(v_hbm.at[pl.ds(b * KB, KB)], vraw.at[s], ksem.at[s, 1]),
        ]

    def kv_start(b):
        @pl.when(b < n)
        def _():
            for d in kv_copies(b):
                d.start()

    qa[:, HD:] = jnp.zeros((heads, qa.shape[1] - HD, rows), BF)
    xcopy.wait()
    a_s[...] = rms(x_s[...])

    def q_step(i, _):
        for d in range(2):
            e = 2 * i + d
            s = ready(e)
            t = dot(a_s[...], ring[s]).astype(BF)
            for j in range(4):
                qa[4 * e + j, 0:HD] = t[:, j * HD:(j + 1) * HD].T
        for d in range(2):
            e = 2 * i + d
            fetch(e + RING, wkv.at[:, col(e + RING - 6)])
        return 0

    lax.fori_loop(0, 3, q_step, 0)
    for b in range(RAW):
        kv_start(b)

    def kv_tiles(e, dst, base):
        for d in range(2):
            s = ready(e + d)
            t = dot(a_s[...], ring[s]).astype(BF)
            for j in range(4):
                dst[base + 4 * d + j] = t[:, j * HD:(j + 1) * HD]

    def k_step(i, _):
        e = 6 + 2 * i
        kv_tiles(e, kn, 8 * i)
        fetch_wo(e + RING, i)
        return 0

    lax.fori_loop(0, 3, k_step, 0)
    kv_tiles(12, vn, 0)
    fetch_wo(24, 3)

    def v_step(i, _):
        e = 14 + 2 * i
        kv_tiles(e, vn, 8 * i + 8)
        fetch_gu(e + RING, i)
        return 0

    lax.fori_loop(0, 2, v_step, 0)

    def bf_round(v):
        return v.astype(BF).astype(F32)

    def set_shift(h, mu):
        mu_s[h] = mu
        first = lax.broadcasted_iota(jnp.int32, (16, rows), 0) == 0
        qa[h, HD:HD + 16] = jnp.where(first, -mu, 0.0).astype(BF)

    vis = lax.broadcasted_iota(jnp.int32, (KB, rows), 0) <= lax.broadcasted_iota(jnp.int32, (KB, rows), 1)

    def local(h, _):
        s = jnp.where(vis, dot(kn[h], qa[h, 0:HD]), FLOOR)
        mu = bf_round(jnp.max(s, axis=0, keepdims=True))
        e = jnp.exp2((s - mu) * c)
        l_s[h] = jnp.sum(e, axis=0, keepdims=True)
        acc[h] = dot(vn[h].T, e.astype(BF))
        set_shift(h, mu)
        return 0

    lax.fori_loop(0, heads, local, 0, unroll=4)

    def exact(h, par):
        s = dot(kt[h], qa[h, 0:HD])
        mo = mu_s[h]
        mu = jnp.maximum(mo, bf_round(jnp.max(s, axis=0, keepdims=True)))
        al = jnp.exp2((mo - mu) * c)
        e = jnp.exp2((s - mu) * c)
        l_s[h] = l_s[h] * al
        acc[h] = acc[h] * al
        lb_s[h] = jnp.sum(e, axis=0, keepdims=True)
        pb[par * heads + h] = e.astype(BF)
        set_shift(h, mu)

    def exact_all(par):
        def one(h, _):
            exact(h, par)
            return 0
        lax.fori_loop(0, heads, one, 0, unroll=2)

    ones = jnp.where(lax.broadcasted_iota(jnp.int32, (KB, HD), 1) == 0, 1.0, 0.0).astype(BF)

    def fast(h, par):
        s = dot(jnp.concatenate([kt[h], ones], axis=1), qa[h])
        e = jnp.exp2(s * c)
        pb[par * heads + h] = e.astype(BF)
        return jnp.sum(e, axis=0, keepdims=True)

    def value(h, par):
        l_s[h] = l_s[h] + lb_s[h]
        acc[h] = acc[h] + dot(vt[h].T, pb[par * heads + h])

    def take(raw, b, dst):
        dst[...] = jnp.swapaxes(raw[lax.rem(b, RAW)], 0, 1)

    @pl.when(n > 0)
    def _():
        for d in kv_copies(0):
            d.wait()
        take(kraw, 0, kt)
        exact_all(0)
        take(vraw, 0, vt)
        kv_start(RAW)

        def block(b, _):
            for d in kv_copies(b):
                d.wait()
            take(kraw, b, kt)
            par = lax.rem(b, 2)

            def group(i, _):
                for g in range(G):
                    value(G * i + g, 1 - par)
                for g in range(G):
                    lb_s[G * i + g] = fast(G * i + g, par)
                return 0

            lax.fori_loop(0, heads // G, group, 0)

            @pl.when(jnp.logical_not(jnp.max(lb_s[...]) <= LIMIT))
            def _():
                exact_all(par)

            take(vraw, b, vt)
            kv_start(b + RAW)
            return 0

        lax.fori_loop(1, n, block, 0)
        last = lax.rem(n - 1, 2)

        def tail(i, _):
            for g in range(G):
                value(G * i + g, last)
            return 0

        lax.fori_loop(0, heads // G, tail, 0)

    for h in range(heads):
        l = l_s[h]
        o_s[:, h * HD:(h + 1) * HD] = (acc[h] * (1.0 / l)).T.astype(BF)
        lse_s[pl.ds(h, 1)] = mu_s[h] * (HD ** -0.5) + jnp.log2(l) * log2
    lcopy = pltpu.make_async_copy(lse_s, lse_hbm, msem.at[1])
    lcopy.start()

    def o_step(nt, _):
        e = 18 + 2 * nt
        s0 = ready(e)
        s1 = ready(e + 1, wo.shape[0] - TK)
        r = dot(o_s[:, 0:TK], ring[s0]) + dot(o_s[:, TK:], ring[s1, pl.ds(0, wo.shape[0] - TK)])
        h_s[:, col(nt)] = (x_s[:, col(nt)].astype(F32) + r).astype(BF)
        fetch_gu(e + RING, nt + 2)
        return 0

    lax.fori_loop(0, 4, o_step, 0)
    a_s[...] = rms(h_s[...])

    def gu_tile(nt):
        s0 = ready(26 + 2 * nt)
        s1 = ready(27 + 2 * nt)
        g = dot(a_s[...], ring[s0])
        u = dot(a_s[...], ring[s1])
        t = (jax.nn.silu(g) * u).astype(BF)
        pb[2 * nt] = t[:, 0:256]
        pb[2 * nt + 1] = t[:, 256:512]

    def gu1(nt, _):
        gu_tile(nt)
        fetch_gu(26 + 2 * nt + RING, nt + 6)
        return 0

    def gu2(nt, _):
        gu_tile(nt)
        fetch_wd(26 + 2 * nt + RING, 2 * (nt - 10))
        return 0

    lax.fori_loop(0, 10, gu1, 0)
    lax.fori_loop(10, 16, gu2, 0)

    def down(nt):
        e = 58 + 4 * nt
        r = h_s[:, col(nt)].astype(F32)
        for kk in range(4):
            s = ready(e + kk)
            lhs = jnp.concatenate([pb[8 * kk + j] for j in range(8)], axis=1)
            r = r + dot(lhs, ring[s])
        y_s[:, col(nt)] = r.astype(BF)
        pltpu.make_async_copy(y_s.at[:, col(nt)], y_hbm.at[:, col(nt)], msem.at[2 + nt]).start()

    down(0)
    fetch_wd(70, 12)
    fetch_wd(72, 14)

    def down_step(nt, _):
        down(nt)
        return 0

    lax.fori_loop(1, 4, down_step, 0)
    lcopy.wait()
    for nt in range(4):
        pltpu.make_async_copy(y_s.at[:, pl.ds(nt * TN, TN)], y_hbm.at[:, pl.ds(nt * TN, TN)], msem.at[2 + nt]).wait()


def layer_call(idx, x, k, v, wq, wkv, wo, wg, wu, wd):
    rows, dm = x.shape
    heads, hd = k.shape[1:]
    vm = pltpu.VMEM
    return pl.pallas_call(
        layer_kernel,
        in_specs=[SM] + [HBM] * 9,
        out_specs=[HBM, HBM],
        out_shape=[jax.ShapeDtypeStruct((rows, dm), BF), jax.ShapeDtypeStruct((heads, rows), F32)],
        scratch_shapes=[
            vm((RING, TK, TN), BF),
            vm((RAW, KB, heads, hd), BF),
            vm((RAW, KB, heads, hd), BF),
            vm((heads, KB, hd), BF),
            vm((heads, KB, hd), BF),
            vm((heads, rows, hd), BF),
            vm((heads, rows, hd), BF),
            vm((heads, 2 * hd, rows), BF),
            vm((heads, hd, rows), F32),
            vm((2 * heads, KB, rows), BF),
            vm((heads, 1, rows), F32),
            vm((heads, 1, rows), F32),
            vm((heads, 1, rows), F32),
            vm((rows, dm), BF),
            vm((rows, dm), BF),
            vm((rows, heads * hd), BF),
            vm((rows, dm), BF),
            vm((rows, dm), BF),
            vm((heads, rows), F32),
            pltpu.SemaphoreType.DMA((RING,)),
            pltpu.SemaphoreType.DMA((RAW, 2)),
            pltpu.SemaphoreType.DMA((6,)),
        ],
        compiler_params=pltpu.CompilerParams(vmem_limit_bytes=67043328),
    )(idx, x, k, v, wq, wkv, wo, wg, wu, wd)


def solution(mesh):
    stages = mesh.shape['pipe']
    next_perm = [(s, (s + 1) % stages) for s in range(stages)]

    def device_step(x, idx, k, v, w_q, w_kv, w_o, w_gate, w_up, w_down):
        y, lse = layer_call(idx, x, k, v, w_q[0], w_kv[0], w_o[0], w_gate[0], w_up[0], w_down[0])
        return lax.ppermute(y, 'pipe', next_perm), lse.T

    rows_spec = P(('data', 'pipe'), None)
    cache_spec = P(('data', 'pipe'), None, None)
    stage_spec = P('pipe', None, None)
    return jax.shard_map(
        device_step,
        mesh=mesh,
        in_specs=(rows_spec, P(('data', 'pipe')), cache_spec, cache_spec) + (stage_spec,) * 6,
        out_specs=(rows_spec, rows_spec),
        check_vma=False,
    )
```

profile of v0, /device:TPU:0, one launch (start us, length us, event | category | flops | bytes accessed | tf_op | source)
XLA Modules:
  0.0 134.7 jit_solution(11765785993152654867)
XLA Ops:
  1.3 117.3 %shard_map.113 = (bf16[256,2048]{1,0:T(8,128)(2,1)}, f32[24,256]{1,0:T(8,128)}) custom-call(s32[1]{0:T(128)S(6)} %copy.13.idx_ref, bf16[256,2048]{1,0:T(8,128)(2,1)} %x_hbm.1, bf16[3840,24,128]{2,1,0:T(8,128)(2,1)} %k_hbm.1, bf16[3840,24,128]{2,1,0:T(8,128)(2,1)} %v_hbm.1, bf16[2048,3072]{1,0:T(8,128)(2,1)} %bitcast.11, bf16[2048,6144]{1,0:T(8,128)(2,1)} %bitcast.10, ...), custom_call_target="tpu_custom_call" | custom-call | tf_op jit(solution)/shard_map/pallas_call | solution.py:298
  118.6 0.0 collective-permute-start
  118.6 15.1 %collective-permute-done = bf16[256,2048]{1,0:T(8,128)(2,1)S(1)} collective-permute-done((bf16[256,2048]{1,0:T(8,128)(2,1)}, bf16[256,2048]{1,0:T(8,128)(2,1)S(1)}, u32[]{:S(2)}, u32[]{:S(2)}) %collective-permute-start) | collective-permute-done | bytes 1048608 | tf_op jit(solution)/shard_map/ppermute | solution.py:337
  133.7 1.0 copy.14
Async XLA Ops:
  118.6 15.1 %collective-permute-start = (bf16[256,2048]{1,0:T(8,128)(2,1)}, bf16[256,2048]{1,0:T(8,128)(2,1)S(1)}, u32[]{:S(2)}, u32[]{:S(2)}) collective-permute-start(bf16[256,2048]{1,0:T(8,128)(2,1)} %get-tuple-element.4), channel_id=1, source_target_pairs={{0,1},{1,2},{2,3},{3,4},{4,5},{5,6},{6,7},{7,0}} | collective-permute-start | bytes 3145736 | tf_op jit(solution)/shard_map/ppermute | solution.py:337
where the time goes:
time: 135 us
  Pallas kernels  117 us (87%)
  waiting for transfers between devices  15.1 us (11%)
    pallas_call x1, Pallas kernels, layer_call(): pl.pallas_call(layer_kernel, in_specs=[SM] + [HBM] * 9, out_specs=[HBM, H...  117 us
    ppermute x1, waiting for transfers between devices, device_step(): return (lax.ppermute(y, 'pipe', next_perm), lse.T)  15.1 us
  transfers between devices with their start and end apart: 1, of which 1 were waited for; matrix products, arithmetic and copies ran while one was open for 0% of the time, Pallas kernels for 0%

commit v1 on v0

--- a/solution.py
+++ b/solution.py
@@ -13,9 +13,9 @@
 TN = 512
 TK = 2048
 RING = 12
-RAW = 3
+KRAW = 3
+VRAW = 4
 KB = 256
-G = 4
 FLOOR = -1e30
 LIMIT = 2.0 ** 15
 HBM = pl.BlockSpec(memory_space=pltpu.HBM)
@@ -31,9 +31,9 @@
     return jnp.dot(a, b, preferred_element_type=F32)
 
 
-def layer_kernel(idx_ref, x_hbm, k_hbm, v_hbm, wq, wkv, wo, wg, wu, wd, y_hbm, lse_hbm,
-                 ring, kraw, vraw, kt, vt, kn, vn, qa, acc, pb, mu_s, l_s, lb_s,
-                 x_s, a_s, o_s, h_s, y_s, lse_s, wsem, ksem, msem):
+def layer_kernel(idx_ref, x_hbm, k_hbm, v_hbm, wq, wkv, wo, wg, wu, t_hbm, h_hbm, lse_hbm,
+                 ring, kraw, vraw, kt, kn, vn, qa, acc, pb, mu_s, l_s, lb_s,
+                 x_s, a_s, o_s, h_s, t_s, lse_s, wsem, ksem, msem, tsem):
     n = idx_ref[0]
     rows, dm = x_s.shape
     heads = qa.shape[0]
@@ -59,11 +59,6 @@
     def fetch_gu(e, nt):
         fetch(e, wg.at[:, col(nt)])
         fetch(e + 1, wu.at[:, col(nt)])
-
-    def fetch_wd(e, j):
-        for d in range(2):
-            jj = j + d
-            fetch(e + d, wd.at[col(lax.rem(jj, 4), TK), col(lax.div(jj, 4))])
 
     xcopy = pltpu.make_async_copy(x_hbm, x_s, msem.at[0])
     xcopy.start()
@@ -73,10 +68,10 @@
         fetch(e, wkv.at[:, pl.ds((e - 6) * TN, TN)])
 
     def kv_copies(b):
-        s = lax.rem(b, RAW)
+        s, t = lax.rem(b, KRAW), lax.rem(b, VRAW)
         return [
-            pltpu.make_async_copy(k_hbm.at[pl.ds(b * KB, KB)], kraw.at[s], ksem.at[s, 0]),
-            pltpu.make_async_copy(v_hbm.at[pl.ds(b * KB, KB)], vraw.at[s], ksem.at[s, 1]),
+            pltpu.make_async_copy(k_hbm.at[pl.ds(b * KB, KB)], kraw.at[s], ksem.at[0, s]),
+            pltpu.make_async_copy(v_hbm.at[pl.ds(b * KB, KB)], vraw.at[t], ksem.at[1, t]),
         ]
 
     def kv_start(b):
@@ -102,8 +97,8 @@
         return 0
 
     lax.fori_loop(0, 3, q_step, 0)
-    for b in range(RAW):
-        kv_start(b)
+    kv_start(0)
+    kv_start(1)
 
     def kv_tiles(e, dst, base):
         for d in range(2):
@@ -149,7 +144,9 @@
         set_shift(h, mu)
         return 0
 
-    lax.fori_loop(0, heads, local, 0, unroll=4)
+    @pl.when(n == 0)
+    def _():
+        lax.fori_loop(0, heads, local, 0, unroll=4)
 
     def exact(h, par):
         s = dot(kt[h], qa[h, 0:HD])
@@ -163,68 +160,69 @@
         pb[par * heads + h] = e.astype(BF)
         set_shift(h, mu)
 
-    def exact_all(par):
+    def exact_all(b, par):
+        kt[...] = jnp.swapaxes(kraw[lax.rem(b, KRAW)], 0, 1)
+
         def one(h, _):
             exact(h, par)
             return 0
         lax.fori_loop(0, heads, one, 0, unroll=2)
 
     ones = jnp.where(lax.broadcasted_iota(jnp.int32, (KB, HD), 1) == 0, 1.0, 0.0).astype(BF)
-
-    def fast(h, par):
-        s = dot(jnp.concatenate([kt[h], ones], axis=1), qa[h])
-        e = jnp.exp2(s * c)
+    k2 = kraw.reshape(KRAW, KB * heads, HD)
+    v2 = vraw.reshape(VRAW, KB * heads, HD)
+
+    def fast(h, par, slot):
+        k = k2.at[slot][pl.ds(h, KB, stride=heads), :]
+        e = jnp.exp2(dot(jnp.concatenate([k, ones], axis=1), qa[h]) * c)
         pb[par * heads + h] = e.astype(BF)
-        return jnp.sum(e, axis=0, keepdims=True)
-
-    def value(h, par):
+        lb_s[h] = jnp.sum(e, axis=0, keepdims=True)
+
+    def value(h, par, slot):
+        v = v2.at[slot][pl.ds(h, KB, stride=heads), :]
         l_s[h] = l_s[h] + lb_s[h]
-        acc[h] = acc[h] + dot(vt[h].T, pb[par * heads + h])
-
-    def take(raw, b, dst):
-        dst[...] = jnp.swapaxes(raw[lax.rem(b, RAW)], 0, 1)
+        acc[h] = acc[h] + dot(v.T, pb[par * heads + h])
+
+    def first(h):
+        q = qa[h, 0:HD]
+        s0 = jnp.where(vis, dot(kn[h], q), FLOOR)
+        s1 = dot(k2.at[0][pl.ds(h, KB, stride=heads), :], q)
+        mu = bf_round(jnp.maximum(jnp.max(s0, axis=0, keepdims=True), jnp.max(s1, axis=0, keepdims=True)))
+        e0 = jnp.exp2((s0 - mu) * c)
+        e1 = jnp.exp2((s1 - mu) * c)
+        l_s[h] = jnp.sum(e0, axis=0, keepdims=True)
+        lb_s[h] = jnp.sum(e1, axis=0, keepdims=True)
+        pb[h] = e1.astype(BF)
+        acc[h] = dot(vn[h].T, e0.astype(BF))
+        set_shift(h, mu)
 
     @pl.when(n > 0)
     def _():
         for d in kv_copies(0):
             d.wait()
-        take(kraw, 0, kt)
-        exact_all(0)
-        take(vraw, 0, vt)
-        kv_start(RAW)
+        kv_start(2)
+        for h in range(heads):
+            first(h)
 
         def block(b, _):
             for d in kv_copies(b):
                 d.wait()
-            take(kraw, b, kt)
+            kv_start(b + 2)
             par = lax.rem(b, 2)
-
-            def group(i, _):
-                for g in range(G):
-                    value(G * i + g, 1 - par)
-                for g in range(G):
-                    lb_s[G * i + g] = fast(G * i + g, par)
-                return 0
-
-            lax.fori_loop(0, heads // G, group, 0)
+            ks, vs = lax.rem(b, KRAW), lax.rem(b - 1, VRAW)
+            for h in range(heads):
+                value(h, 1 - par, vs)
+                fast(h, par, ks)
 
             @pl.when(jnp.logical_not(jnp.max(lb_s[...]) <= LIMIT))
             def _():
-                exact_all(par)
-
-            take(vraw, b, vt)
-            kv_start(b + RAW)
+                exact_all(b, par)
+
             return 0
 
         lax.fori_loop(1, n, block, 0)
-        last = lax.rem(n - 1, 2)
-
-        def tail(i, _):
-            for g in range(G):
-                value(G * i + g, last)
-            return 0
-
-        lax.fori_loop(0, heads // G, tail, 0)
+        for h in range(heads):
+            value(h, lax.rem(n - 1, 2), lax.rem(n - 1, VRAW))
 
     for h in range(heads):
         l = l_s[h]
@@ -245,14 +243,19 @@
     lax.fori_loop(0, 4, o_step, 0)
     a_s[...] = rms(h_s[...])
 
+    hcopy = pltpu.make_async_copy(h_s, h_hbm, msem.at[2])
+    hcopy.start()
+
+    def t_copy(nt):
+        return pltpu.make_async_copy(t_s.at[:, col(nt)], t_hbm.at[:, col(nt)], tsem.at[nt])
+
     def gu_tile(nt):
         s0 = ready(26 + 2 * nt)
         s1 = ready(27 + 2 * nt)
         g = dot(a_s[...], ring[s0])
         u = dot(a_s[...], ring[s1])
-        t = (jax.nn.silu(g) * u).astype(BF)
-        pb[2 * nt] = t[:, 0:256]
-        pb[2 * nt + 1] = t[:, 256:512]
+        t_s[:, col(nt)] = (jax.nn.silu(g) * u).astype(BF)
+        t_copy(nt).start()
 
     def gu1(nt, _):
         gu_tile(nt)
@@ -261,50 +264,107 @@
 
     def gu2(nt, _):
         gu_tile(nt)
-        fetch_wd(26 + 2 * nt + RING, 2 * (nt - 10))
+        return 0
+
+    def drain(nt, _):
+        t_copy(nt).wait()
         return 0
 
     lax.fori_loop(0, 10, gu1, 0)
     lax.fori_loop(10, 16, gu2, 0)
-
-    def down(nt):
-        e = 58 + 4 * nt
-        r = h_s[:, col(nt)].astype(F32)
-        for kk in range(4):
-            s = ready(e + kk)
-            lhs = jnp.concatenate([pb[8 * kk + j] for j in range(8)], axis=1)
-            r = r + dot(lhs, ring[s])
-        y_s[:, col(nt)] = r.astype(BF)
-        pltpu.make_async_copy(y_s.at[:, col(nt)], y_hbm.at[:, col(nt)], msem.at[2 + nt]).start()
-
-    down(0)
-    fetch_wd(70, 12)
-    fetch_wd(72, 14)
-
-    def down_step(nt, _):
-        down(nt)
-        return 0
-
-    lax.fori_loop(1, 4, down_step, 0)
     lcopy.wait()
-    for nt in range(4):
-        pltpu.make_async_copy(y_s.at[:, pl.ds(nt * TN, TN)], y_hbm.at[:, pl.ds(nt * TN, TN)], msem.at[2 + nt]).wait()
-
-
-def layer_call(idx, x, k, v, wq, wkv, wo, wg, wu, wd):
+    hcopy.wait()
+    lax.fori_loop(0, 16, drain, 0)
+
+
+def down_kernel(stages, t_hbm, h_hbm, wd, y_hbm, w_s, t_s, h_s, y_s, wsem, tsem, hsem, send, recv):
+    me = lax.axis_index('pipe')
+    nxt = lax.rem(me + 1, stages)
+    prev = lax.rem(me + stages - 1, stages)
+    chunks = w_s.shape[0]
+    parts = t_s.shape[0]
+    width = w_s.shape[2]
+    depth = t_s.shape[2]
+    barrier = pltpu.get_barrier_semaphore()
+    pl.semaphore_signal(barrier, inc=1, device_id={'pipe': prev}, device_id_type=pl.DeviceIdType.MESH)
+
+    def wcopy(i, k):
+        return pltpu.make_async_copy(
+            wd.at[pl.ds(k * depth, depth), pl.ds(i * width, width)], w_s.at[i, pl.ds(k * depth, depth)], wsem.at[i, k])
+
+    tcopies = [pltpu.make_async_copy(t_hbm.at[:, pl.ds(k * depth, depth)], t_s.at[k], tsem.at[k]) for k in range(parts)]
+    hcopy = pltpu.make_async_copy(h_hbm, h_s, hsem)
+    for k in range(parts):
+        tcopies[k].start()
+        wcopy(0, k).start()
+        if k == 0:
+            hcopy.start()
+    for i in range(1, chunks):
+        for k in range(parts):
+            wcopy(i, k).start()
+
+    def out(i):
+        cols = pl.ds(i * width, width)
+        return pltpu.make_async_remote_copy(
+            src_ref=y_s.at[:, cols], dst_ref=y_hbm.at[:, cols], send_sem=send.at[i], recv_sem=recv.at[i],
+            device_id={'pipe': nxt}, device_id_type=pl.DeviceIdType.MESH)
+
+    hcopy.wait()
+    for i in range(chunks):
+        cols = pl.ds(i * width, width)
+        r = h_s[:, cols].astype(F32)
+        for k in range(parts):
+            if i == 0:
+                tcopies[k].wait()
+            wcopy(i, k).wait()
+            r = r + dot(t_s[k], w_s[i, pl.ds(k * depth, depth)])
+        y_s[:, cols] = r.astype(BF)
+        if i == 0:
+            pl.semaphore_wait(barrier, 1)
+        out(i).start()
+    for i in range(chunks):
+        out(i).wait()
+
+
+def down_call(t, h, wd, stages, width=256, parts=4):
+    rows, dm = h.shape
+    ff = t.shape[1]
+    chunks = dm // width
+    vm = pltpu.VMEM
+    return pl.pallas_call(
+        lambda *r: down_kernel(stages, *r),
+        in_specs=[HBM] * 3,
+        out_specs=HBM,
+        out_shape=jax.ShapeDtypeStruct((rows, dm), BF),
+        scratch_shapes=[
+            vm((chunks, ff, width), BF),
+            vm((parts, rows, ff // parts), BF),
+            vm((rows, dm), BF),
+            vm((rows, dm), BF),
+            pltpu.SemaphoreType.DMA((chunks, parts)),
+            pltpu.SemaphoreType.DMA((parts,)),
+            pltpu.SemaphoreType.DMA,
+            pltpu.SemaphoreType.DMA((chunks,)),
+            pltpu.SemaphoreType.DMA((chunks,)),
+        ],
+        compiler_params=pltpu.CompilerParams(vmem_limit_bytes=60 * 2**20, collective_id=0, has_side_effects=True),
+    )(t, h, wd)
+
+
+def layer_call(idx, x, k, v, wq, wkv, wo, wg, wu, wd=None):
     rows, dm = x.shape
+    ff = wg.shape[1]
     heads, hd = k.shape[1:]
     vm = pltpu.VMEM
     return pl.pallas_call(
         layer_kernel,
-        in_specs=[SM] + [HBM] * 9,
-        out_specs=[HBM, HBM],
-        out_shape=[jax.ShapeDtypeStruct((rows, dm), BF), jax.ShapeDtypeStruct((heads, rows), F32)],
+        in_specs=[SM] + [HBM] * 8,
+        out_specs=[HBM] * 3,
+        out_shape=[jax.ShapeDtypeStruct((rows, ff), BF), jax.ShapeDtypeStruct((rows, dm), BF), jax.ShapeDtypeStruct((heads, rows), F32)],
         scratch_shapes=[
             vm((RING, TK, TN), BF),
-            vm((RAW, KB, heads, hd), BF),
-            vm((RAW, KB, heads, hd), BF),
-            vm((heads, KB, hd), BF),
+            vm((KRAW, KB, heads, hd), BF),
+            vm((VRAW, KB, heads, hd), BF),
             vm((heads, KB, hd), BF),
             vm((heads, rows, hd), BF),
             vm((heads, rows, hd), BF),
@@ -318,23 +378,23 @@
             vm((rows, dm), BF),
             vm((rows, heads * hd), BF),
             vm((rows, dm), BF),
-            vm((rows, dm), BF),
+            vm((rows, ff), BF),
             vm((heads, rows), F32),
             pltpu.SemaphoreType.DMA((RING,)),
-            pltpu.SemaphoreType.DMA((RAW, 2)),
-            pltpu.SemaphoreType.DMA((6,)),
+            pltpu.SemaphoreType.DMA((2, VRAW)),
+            pltpu.SemaphoreType.DMA((3,)),
+            pltpu.SemaphoreType.DMA((16,)),
         ],
         compiler_params=pltpu.CompilerParams(vmem_limit_bytes=67043328),
-    )(idx, x, k, v, wq, wkv, wo, wg, wu, wd)
+    )(idx, x, k, v, wq, wkv, wo, wg, wu)
 
 
 def solution(mesh):
     stages = mesh.shape['pipe']
-    next_perm = [(s, (s + 1) % stages) for s in range(stages)]
 
     def device_step(x, idx, k, v, w_q, w_kv, w_o, w_gate, w_up, w_down):
-        y, lse = layer_call(idx, x, k, v, w_q[0], w_kv[0], w_o[0], w_gate[0], w_up[0], w_down[0])
-        return lax.ppermute(y, 'pipe', next_perm), lse.T
+        t, h, lse = layer_call(idx, x, k, v, w_q[0], w_kv[0], w_o[0], w_gate[0], w_up[0])
+        return down_call(t, h, w_down[0], stages), lse.T
 
     rows_spec = P(('data', 'pipe'), None)
     cache_spec = P(('data', 'pipe'), None, None)

time: 135 us -> 126 us (0.933)
  the two profiles are of different devices: /device:TPU:0 before, /device:TPU:4 now
where the time goes in v1:
time: 126 us; the launch traced here: 125 us
  Pallas kernels  122 us (97%)
  local copies, waits for them, and re-layouts  2.3 us (2%)
  between operations  1.29 us (1%)
    pallas_call x1, Pallas kernels, layer_call(): pl.pallas_call(layer_kernel, in_specs=[SM] + [HBM] * 8, out_specs=[HBM] *...  88.9 us
    pallas_call x1, Pallas kernels, down_call(): pl.pallas_call(lambda *r: down_kernel(stages, *r), in_specs=[HBM] * 3, ou...  32.9 us

profile of v1, /device:TPU:4, one launch (start us, length us, event | category | flops | bytes accessed | tf_op | source)
XLA Modules:
  0.0 125.5 jit_solution(749971945165924190)
XLA Ops:
  1.3 88.9 %shard_map.113 = (bf16[256,8192]{1,0:T(8,128)(2,1)}, bf16[256,2048]{1,0:T(8,128)(2,1)}, f32[24,256]{1,0:T(8,128)}) custom-call(s32[1]{0:T(128)S(6)} %copy.13.idx_ref, bf16[256,2048]{1,0:T(8,128)(2,1)} %x_hbm.1, bf16[3840,24,128]{2,1,0:T(8,128)(2,1)} %k_hbm.1, bf16[3840,24,128]{2,1,0:T(8,128)(2,1)} %v_hbm.1, bf16[2048,3072]{1,0:T(8,128)(2,1)} %bitcast.11, ...), custom_call_target="tpu_custom_call" | custom-call | tf_op jit(solution)/shard_map/pallas_call | solution.py:359
  90.2 32.9 %shard_map.114 = bf16[256,2048]{1,0:T(8,128)(2,1)} custom-call(bf16[256,8192]{1,0:T(8,128)(2,1)} %get-tuple-element.5.r_0_, bf16[256,2048]{1,0:T(8,128)(2,1)} %get-tuple-element.6.r_1_, bf16[8192,2048]{1,0:T(8,128)(2,1)} %bitcast.9), custom_call_target="tpu_custom_call" | custom-call | tf_op jit(solution)/shard_map/pallas_call | solution.py:334
  123.1 2.3 %copy.14 = bf16[256,2048]{1,0:T(8,128)(2,1)} copy(bf16[256,2048]{1,0:T(8,128)(2,1)} %shard_map.114) | data formatting | bytes 2097152

commit v2 on v1

--- a/solution.py
+++ b/solution.py
@@ -13,6 +13,7 @@
 TN = 512
 TK = 2048
 RING = 12
+AHEAD = 4
 KRAW = 3
 VRAW = 4
 KB = 256
@@ -60,12 +61,31 @@
         fetch(e, wg.at[:, col(nt)])
         fetch(e + 1, wu.at[:, col(nt)])
 
+    def fetch_mid(e):
+        rest = wo.shape[0] - TK
+        even = lax.rem(e, 2) == 0
+        nt = lax.div(e - 18, 2)
+
+        @pl.when(jnp.logical_and(e < 26, even))
+        def _():
+            fetch(e, wo.at[pl.ds(0, TK), col(nt)])
+
+        @pl.when(jnp.logical_and(e < 26, jnp.logical_not(even)))
+        def _():
+            fetch(e, wo.at[pl.ds(TK, rest), col(nt)], rest)
+
+        @pl.when(jnp.logical_and(e >= 26, even))
+        def _():
+            fetch(e, wg.at[:, col(nt - 4)])
+
+        @pl.when(jnp.logical_and(e >= 26, jnp.logical_not(even)))
+        def _():
+            fetch(e, wu.at[:, col(nt - 4)])
+
     xcopy = pltpu.make_async_copy(x_hbm, x_s, msem.at[0])
     xcopy.start()
-    for e in range(6):
+    for e in range(AHEAD):
         fetch(e, wq.at[:, pl.ds(e * TN, TN)])
-    for e in range(6, RING):
-        fetch(e, wkv.at[:, pl.ds((e - 6) * TN, TN)])
 
     def kv_copies(b):
         s, t = lax.rem(b, KRAW), lax.rem(b, VRAW)
@@ -85,20 +105,29 @@
     a_s[...] = rms(x_s[...])
 
     def q_step(i, _):
+        @pl.when(i == 0)
+        def _():
+            for d in range(AHEAD, 6):
+                fetch(d, wq.at[:, pl.ds(d * TN, TN)])
+
+        @pl.when(i > 0)
+        def _():
+            for d in range(2):
+                fetch(2 * i + AHEAD + d, wkv.at[:, col(2 * i + AHEAD + d - 6)])
+
         for d in range(2):
             e = 2 * i + d
             s = ready(e)
             t = dot(a_s[...], ring[s]).astype(BF)
             for j in range(4):
                 qa[4 * e + j, 0:HD] = t[:, j * HD:(j + 1) * HD].T
+        return 0
+
+    lax.fori_loop(0, 3, q_step, 0)
+
+    def fetch_kv(e):
         for d in range(2):
-            e = 2 * i + d
-            fetch(e + RING, wkv.at[:, col(e + RING - 6)])
-        return 0
-
-    lax.fori_loop(0, 3, q_step, 0)
-    kv_start(0)
-    kv_start(1)
+            fetch(e + d, wkv.at[:, col(e + d - 6)])
 
     def kv_tiles(e, dst, base):
         for d in range(2):
@@ -109,18 +138,20 @@
 
     def k_step(i, _):
         e = 6 + 2 * i
+        fetch_kv(e + AHEAD)
         kv_tiles(e, kn, 8 * i)
-        fetch_wo(e + RING, i)
         return 0
 
     lax.fori_loop(0, 3, k_step, 0)
+    fetch_kv(12 + AHEAD)
+    kv_start(0)
+    kv_start(1)
     kv_tiles(12, vn, 0)
-    fetch_wo(24, 3)
 
     def v_step(i, _):
         e = 14 + 2 * i
+        fetch_wo(e + AHEAD, i)
         kv_tiles(e, vn, 8 * i + 8)
-        fetch_gu(e + RING, i)
         return 0
 
     lax.fori_loop(0, 2, v_step, 0)
@@ -208,6 +239,11 @@
             for d in kv_copies(b):
                 d.wait()
             kv_start(b + 2)
+
+            @pl.when(b <= 8)
+            def _():
+                fetch_mid(21 + b)
+
             par = lax.rem(b, 2)
             ks, vs = lax.rem(b, KRAW), lax.rem(b - 1, VRAW)
             for h in range(heads):
@@ -224,6 +260,11 @@
         for h in range(heads):
             value(h, lax.rem(n - 1, 2), lax.rem(n - 1, VRAW))
 
+    def late(e, _):
+        fetch_mid(e)
+        return 0
+
+    lax.fori_loop(22 + jnp.clip(n - 1, 0, 8), 30, late, 0)
     for h in range(heads):
         l = l_s[h]
         o_s[:, h * HD:(h + 1) * HD] = (acc[h] * (1.0 / l)).T.astype(BF)
@@ -299,7 +340,8 @@
         wcopy(0, k).start()
         if k == 0:
             hcopy.start()
-    for i in range(1, chunks):
+    ahead = 2
+    for i in range(1, ahead):
         for k in range(parts):
             wcopy(i, k).start()
 
@@ -312,12 +354,14 @@
     hcopy.wait()
     for i in range(chunks):
         cols = pl.ds(i * width, width)
-        r = h_s[:, cols].astype(F32)
         for k in range(parts):
             if i == 0:
                 tcopies[k].wait()
             wcopy(i, k).wait()
-            r = r + dot(t_s[k], w_s[i, pl.ds(k * depth, depth)])
+        if i + ahead < chunks:
+            for k in range(parts):
+                wcopy(i + ahead, k).start()
+        r = h_s[:, cols].astype(F32) + dot(jnp.concatenate([t_s[k] for k in range(parts)], axis=1), w_s[i])
         y_s[:, cols] = r.astype(BF)
         if i == 0:
             pl.semaphore_wait(barrier, 1)
@@ -334,7 +378,7 @@
     return pl.pallas_call(
         lambda *r: down_kernel(stages, *r),
         in_specs=[HBM] * 3,
-        out_specs=HBM,
+        out_specs=pl.BlockSpec(memory_space=pltpu.VMEM),
         out_shape=jax.ShapeDtypeStruct((rows, dm), BF),
         scratch_shapes=[
             vm((chunks, ff, width), BF),
@@ -347,7 +391,7 @@
             pltpu.SemaphoreType.DMA((chunks,)),
             pltpu.SemaphoreType.DMA((chunks,)),
         ],
-        compiler_params=pltpu.CompilerParams(vmem_limit_bytes=60 * 2**20, collective_id=0, has_side_effects=True),
+        compiler_params=pltpu.CompilerParams(vmem_limit_bytes=48 * 2**20, collective_id=0, has_side_effects=True),
     )(t, h, wd)
 
 

time: 126 us -> 113 us (0.90)
  the two profiles are of different devices: /device:TPU:4 before, /device:TPU:6 now
where the time goes in v2:
time: 113 us; the launch traced here: 112 us
  Pallas kernels  109 us (96%)
  local copies, waits for them, and re-layouts  2.19 us (2%)
  between operations  1.3 us (1%)
    pallas_call x1, Pallas kernels, layer_call(): pl.pallas_call(layer_kernel, in_specs=[SM] + [HBM] * 8, out_specs=[HBM] *...  84.1 us
    pallas_call x1, Pallas kernels, down_call(): pl.pallas_call(lambda *r: down_kernel(stages, *r), in_specs=[HBM] * 3, ou...  24.5 us

profile of v2, /device:TPU:6, one launch (start us, length us, event | category | flops | bytes accessed | tf_op | source)
XLA Modules:
  0.0 112.1 jit_solution(15109692208649091971)
XLA Ops:
  1.3 84.1 %shard_map.113 = (bf16[256,8192]{1,0:T(8,128)(2,1)}, bf16[256,2048]{1,0:T(8,128)(2,1)}, f32[24,256]{1,0:T(8,128)}) custom-call(s32[1]{0:T(128)S(6)} %copy.13.idx_ref, bf16[256,2048]{1,0:T(8,128)(2,1)} %x_hbm.1, bf16[3840,24,128]{2,1,0:T(8,128)(2,1)} %k_hbm.1, bf16[3840,24,128]{2,1,0:T(8,128)(2,1)} %v_hbm.1, bf16[2048,3072]{1,0:T(8,128)(2,1)} %bitcast.11, ...), custom_call_target="tpu_custom_call" | custom-call | tf_op jit(solution)/shard_map/pallas_call | solution.py:403
  85.4 0.0 copy-start
  85.4 1.2 %copy-done = bf16[256,2048]{1,0:T(8,128)(2,1)S(1)} copy-done((bf16[256,2048]{1,0:T(8,128)(2,1)S(1)}, bf16[256,2048]{1,0:T(8,128)(2,1)}, u32[]{:S(2)}) %copy-start) | copy-done | bytes 1048600
  86.6 24.5 %shard_map.114 = bf16[256,2048]{1,0:T(8,128)(2,1)S(1)} custom-call(bf16[256,8192]{1,0:T(8,128)(2,1)} %get-tuple-element.5.r_0_, bf16[256,2048]{1,0:T(8,128)(2,1)S(1)} %copy-done, bf16[8192,2048]{1,0:T(8,128)(2,1)} %bitcast.9), custom_call_target="tpu_custom_call" | custom-call | tf_op jit(solution)/shard_map/pallas_call | solution.py:378
  111.1 1.0 copy.14
Async XLA Ops:
  85.4 1.2 %copy-start = (bf16[256,2048]{1,0:T(8,128)(2,1)S(1)}, bf16[256,2048]{1,0:T(8,128)(2,1)}, u32[]{:S(2)}) copy-start(bf16[256,2048]{1,0:T(8,128)(2,1)} %get-tuple-element.6.r_1_) | copy-start | bytes 3145732
